TPU v7x, 32 devices: a whole 2x2x4 slice. The times are simulated.
32 devices in a mesh: ctx: 8 (over y, x, core), head: 4 (over z).
Axes of the slice: x: 2, y: 2, z: 4, core: 2. Of those that a mesh axis runs over, the one named last changes fastest.
Arguments:
- tokens: bfloat16 [2, 2048, 2048], P(None, 'ctx'), may hold values from -6 to 6
- w_qkv: bfloat16 [2048, 4, 1536], P(None, 'head'), as said below
- w_rate: bfloat16 [2048, 4], P(None, 'head'), may hold values from -0.125 to 0.125
- w_out: bfloat16 [4, 512, 2048], P('head'), may hold values from -0.125 to 0.125
- fw_gain: float32 [4, 512], P('head'), may hold values from 0.25 to 1.75
- fast_first: float32 [4, 512, 512], P('head'), may hold values from -0.25 to 0.25
- fast_third: float32 [4, 512, 512], P('head'), may hold values from -0.25 to 0.25
- fast_second: float32 [4, 512, 512], P('head'), may hold values from -0.25 to 0.25
Outputs:
- mixed: bfloat16 [2, 2048, 2048], P(None, 'ctx', 'head')
- new_first: float32 [4, 512, 512], P('head')
- new_third: float32 [4, 512, 512], P('head')
- new_second: float32 [4, 512, 512], P('head')
Inputs may be any that keep to these rules, and one draw needn't show every extreme that they name: `w_qkv`: A projection scaled by its fan-in 2048.
All inputs are finite; a program needn't handle non-finite values.
Results may differ from a plain program's by a relative error of at most 0.039.
Values may be sent and summed in bfloat16 or wider, within the bound.
A program may use at most 128 MiB of HBM per device.

v0:
```python
import jax
import jax.numpy as jnp
from jax import lax
from jax.sharding import PartitionSpec as P

WINDOW = 2048
NS_STEPS = 5


coeff_a = 3.4445
coeff_b = -4.775
coeff_c = 2.0315
fast_step = 0.5
norm_eps = 1e-06


def passed_along(value, axis, steps):
    count = lax.axis_size(axis)
    pairs = [(source, (source + steps) % count) for source in range(count)]
    return lax.ppermute(value, axis, pairs)


def inner_rows(left, right):
    return lax.dot_general(
        left, right, (((0,), (0,)), ((), ())), preferred_element_type=jnp.float32
    )


def silu_grad(hidden):
    sigma = jax.nn.sigmoid(hidden)
    return sigma * (1.0 + hidden * (1.0 - sigma))


def narrow(weights):
    return tuple((weight.astype(jnp.bfloat16) for weight in weights))


def fast_apply(queries, narrowed):
    hidden_one = jnp.dot(queries, narrowed[0], preferred_element_type=jnp.float32)
    hidden_three = jnp.dot(queries, narrowed[1], preferred_element_type=jnp.float32)
    activ = (jax.nn.silu(hidden_one) * hidden_three).astype(jnp.bfloat16)
    return jnp.dot(activ, narrowed[2], preferred_element_type=jnp.float32)


def fast_grads(keys, values, rates, narrowed):
    hidden_one = jnp.dot(keys, narrowed[0], preferred_element_type=jnp.float32)
    hidden_three = jnp.dot(keys, narrowed[1], preferred_element_type=jnp.float32)
    activ = (jax.nn.silu(hidden_one) * hidden_three).astype(jnp.bfloat16)
    target = (-rates[:, None] * values.astype(jnp.float32)).astype(jnp.bfloat16)
    grad_second = inner_rows(activ, target)
    dactiv = lax.dot_general(
        target, narrowed[2], (((1,), (1,)), ((), ())), preferred_element_type=jnp.float32
    )
    d_first = (dactiv * hidden_three * silu_grad(hidden_one)).astype(jnp.bfloat16)
    d_third = (dactiv * jax.nn.silu(hidden_one)).astype(jnp.bfloat16)
    return (inner_rows(keys, d_first), inner_rows(keys, d_third), grad_second)


def gram_of(current):
    return lax.dot_general(
        current,
        current,
        (((0,), (0,)), ((), ())),
        precision=lax.Precision.HIGHEST,
        preferred_element_type=jnp.float32,
    )


def ns_update(current, gram):
    poly = coeff_b * gram + coeff_c * jnp.dot(gram, gram, precision=lax.Precision.HIGHEST)
    return coeff_a * current + jnp.dot(current, poly, precision=lax.Precision.HIGHEST)


def orthogonalize(grad):
    current = grad / jnp.sqrt(jnp.sum(grad * grad) + norm_eps)
    for step_num in range(NS_STEPS):
        current = ns_update(current, gram_of(current))
    return current


def window_softmax(query_rows, key_rows, value_rows, first_key):
    row_count = query_rows.shape[0]
    key_span = key_rows.shape[0]
    window_len = key_span - row_count
    scores = lax.dot_general(
        query_rows, key_rows, (((1,), (1,)), ((), ())), preferred_element_type=jnp.float32
    )
    scores = scores * query_rows.shape[1] ** (-0.5)
    offsets = (
        window_len
        + lax.broadcasted_iota(jnp.int32, (row_count, key_span), 0)
        - lax.broadcasted_iota(jnp.int32, (row_count, key_span), 1)
    )
    positions = first_key + lax.broadcasted_iota(jnp.int32, (row_count, key_span), 1)
    allowed = (offsets >= 0) & (offsets < window_len) & (positions >= 0)
    scores = jnp.where(allowed, scores, -1e30)
    highest = jnp.max(scores, axis=1, keepdims=True)
    weights = jnp.exp(scores - highest)
    weights = (weights / jnp.sum(weights, axis=1, keepdims=True)).astype(jnp.bfloat16)
    return jnp.dot(weights, value_rows, preferred_element_type=jnp.float32)


def update_weights(grads):
    totals = (
        lax.psum(grads[0].astype(jnp.bfloat16), "ctx").astype(jnp.float32),
        lax.psum(grads[1].astype(jnp.bfloat16), "ctx").astype(jnp.float32),
        lax.psum(grads[2].astype(jnp.bfloat16), "ctx").astype(jnp.float32),
    )
    return tuple((orthogonalize(total) for total in totals))


def shards(tokens, w_qkv, w_rate, w_out, fw_gain, fast_first, fast_third, fast_second):
    block_count, tok_rows, width = tokens.shape
    head_dim = w_out.shape[1]
    ctx_size = lax.axis_size("ctx")
    ctx_index = lax.axis_index("ctx")
    flat = tokens.reshape(block_count * tok_rows, width)
    projected = jnp.dot(
        flat, w_qkv.reshape(width, 3 * head_dim), preferred_element_type=jnp.float32
    ).astype(jnp.bfloat16)
    projected = projected.reshape(block_count, tok_rows, 3, head_dim)
    rates = jax.nn.softplus(jnp.dot(flat, w_rate, preferred_element_type=jnp.float32)).reshape(
        block_count, tok_rows
    )
    queries = projected[:, :, 0]
    keys = projected[:, :, 1]
    values = projected[:, :, 2]
    stacked = jnp.stack([keys, values])
    reach = WINDOW // tok_rows
    received = []
    moving = stacked
    for distance in range(1, reach + 1):
        moving = passed_along(moving, "ctx", 1)
        received.append(moving)
    attended = []
    for block_num in range(block_count):
        key_blocks = []
        value_blocks = []
        for distance in range(reach, 0, -1):
            piece = received[distance - 1]
            if block_num == 0:
                chosen = piece[:, 0]
            else:
                chosen = jnp.where(
                    ctx_index >= distance, piece[:, block_num], piece[:, block_num - 1]
                )
            key_blocks.append(chosen[0])
            value_blocks.append(chosen[1])
        key_blocks.append(keys[block_num])
        value_blocks.append(values[block_num])
        first_key = block_num * tok_rows * ctx_size + ctx_index * tok_rows - WINDOW
        attended.append(
            window_softmax(
                queries[block_num],
                jnp.concatenate(key_blocks, axis=0),
                jnp.concatenate(value_blocks, axis=0),
                first_key,
            )
        )
    current = (fast_first[0], fast_third[0], fast_second[0])
    outputs = []
    for block_num in range(block_count):
        outputs.append(fast_apply(queries[block_num], narrow(current)))
        if block_num + 1 < block_count:
            grads = fast_grads(
                keys[block_num], values[block_num], rates[block_num], narrow(current)
            )
            updates = update_weights(grads)
            current = tuple(
                (weight - fast_step * update for weight, update in zip(current, updates))
            )
    fast_out = jnp.stack(outputs)
    normed = (
        fast_out
        * lax.rsqrt(jnp.mean(fast_out * fast_out, axis=2, keepdims=True) + norm_eps)
        * fw_gain[0]
    )
    combined = (jnp.stack(attended) + normed).astype(jnp.bfloat16)
    terms = jnp.dot(
        combined.reshape(block_count * tok_rows, head_dim),
        w_out[0],
        preferred_element_type=jnp.float32,
    )
    terms = terms.reshape(block_count, tok_rows, width)
    mixed = lax.psum_scatter(terms.astype(jnp.bfloat16), "head", scatter_dimension=2, tiled=True)
    return (mixed, current[0][None], current[1][None], current[2][None])


def solution(mesh):
    placed = (
        P(None, "ctx", None),
        P(None, "head", None),
        P(None, "head"),
        P("head", None, None),
        P("head", None),
        P("head", None, None),
        P("head", None, None),
        P("head", None, None),
    )
    return jax.shard_map(
        shards,
        mesh=mesh,
        in_specs=placed,
        out_specs=(
            P(None, "ctx", "head"),
            P("head", None, None),
            P("head", None, None),
            P("head", None, None),
        ),
        check_vma=False,
    )
```

profile of v0, /device:TPU:0, one launch (start us, length us, event | category | flops | bytes accessed | tf_op | source)
XLA Modules:
  0.0 361.7 jit_solution(9130644076995065237)
XLA Ops:
  8.8 7.3 %fusion.4 = bf16[512,1536]{1,0:T(8,128)(2,1)} fusion(bf16[512,2048]{1,0:T(8,128)(2,1)S(1)} %bitcast.286, bf16[2048,1,1536]{2,0,1:T(8,128)(2,1)} %param.9), kind=kOutput, calls=%fused_computation.6 | convolution fusion | flops 3222011904 | bytes 9961472 | tf_op jit(solution)/shard_map/dot_general | solution.py:118
  16.0 2.6 copy.1209
  18.6 3.5 reshape.210
  22.1 2.0 slice_bitcast_fusion.1
  24.2 2.5 pad_maximum_fusion
  27.2 3.5 fusion.114
  31.5 2.0 copy.1309
  39.5 2.0 copy.1241
  44.3 2.4 convolution_bitcast_fusion.1
  46.7 54.5 %all-reduce.3.cloned.1.call-done = (bf16[512,512]{1,0:T(8,128)(2,1)}, bf16[512,512]{1,0:T(8,128)(2,1)}, bf16[512,512]{1,0:T(8,128)(2,1)}) async-done(((bf16[512,512]{1,0:T(8,128)(2,1)}, bf16[512,512]{1,0:T(8,128)(2,1)}, bf16[512,512]{1,0:T(8,128)(2,1)}), (bf16[512,512]{1,0:T(8,128)(2,1)}, bf16[512,512]{1,0:T(8,128)(2,1)}, bf16[512,512]{1,0:T(8,128)(2,1)})) %all-reduce.3.cloned.1.call-update) | async-done | bytes 1572880 | tf_op jit(solution)/shard_map/psum | solution.py:107
  103.8 3.1 fusion.44
  116.4 2.1 fusion.145
  129.7 2.1 fusion.14
  142.9 2.3 convolution_add_fusion.8
  156.5 2.0 fusion.143
  158.5 2.9 fusion.20
  171.6 2.1 convolution_add_fusion.13
  185.1 2.3 fusion.139
  191.5 2.9 fusion.32
  196.3 6.6 %collective-permute-done.1 = bf16[2,2,256,512]{2,1,3,0:T(2,128)(2,1)} collective-permute-done((bf16[2,2,256,512]{2,1,3,0:T(2,128)(2,1)}, bf16[2,2,256,512]{2,1,3,0:T(2,128)(2,1)}, u32[]{:S(2)}, u32[]{:S(2)}) %collective-permute-start.1) | collective-permute-done | bytes 1048608 | tf_op jit(solution)/shard_map/ppermute | solution.py:20
  204.0 2.8 convolution_bitcast_fusion
  208.2 3.3 broadcast_select_fusion
  211.5 6.8 %collective-permute-done.2 = bf16[2,2,256,512]{2,1,3,0:T(2,128)(2,1)S(1)} collective-permute-done((bf16[2,2,256,512]{2,1,3,0:T(2,128)(2,1)}, bf16[2,2,256,512]{2,1,3,0:T(2,128)(2,1)S(1)}, u32[]{:S(2)}, u32[]{:S(2)}) %collective-permute-start.2) | collective-permute-done | bytes 1048608 | tf_op jit(solution)/shard_map/ppermute | solution.py:20
  221.4 3.3 broadcast_select_fusion.1
  225.8 7.7 %collective-permute-done.3 = bf16[2,2,256,512]{2,1,3,0:T(2,128)(2,1)S(1)} collective-permute-done((bf16[2,2,256,512]{2,1,3,0:T(2,128)(2,1)S(1)}, bf16[2,2,256,512]{2,1,3,0:T(2,128)(2,1)S(1)}, u32[]{:S(2)}, u32[]{:S(2)}) %collective-permute-start.3) | collective-permute-done | bytes 1048608 | tf_op jit(solution)/shard_map/ppermute | solution.py:20
  239.1 9.6 %collective-permute-done.4 = bf16[2,2,256,512]{2,1,3,0:T(2,128)(2,1)S(1)} collective-permute-done((bf16[2,2,256,512]{2,1,3,0:T(2,128)(2,1)S(1)}, bf16[2,2,256,512]{2,1,3,0:T(2,128)(2,1)S(1)}, u32[]{:S(2)}, u32[]{:S(2)}) %collective-permute-start.4) | collective-permute-done | bytes 1048608 | tf_op jit(solution)/shard_map/ppermute | solution.py:20
  254.1 9.7 %collective-permute-done.5 = bf16[2,2,256,512]{2,1,3,0:T(2,128)(2,1)S(1)} collective-permute-done((bf16[2,2,256,512]{2,1,3,0:T(2,128)(2,1)S(1)}, bf16[2,2,256,512]{2,1,3,0:T(2,128)(2,1)S(1)}, u32[]{:S(2)}, u32[]{:S(2)}) %collective-permute-start.5) | collective-permute-done | bytes 1048608 | tf_op jit(solution)/shard_map/ppermute | solution.py:20
  268.7 10.4 %collective-permute-done.6 = bf16[2,2,256,512]{2,1,3,0:T(2,128)(2,1)S(1)} collective-permute-done((bf16[2,2,256,512]{2,1,3,0:T(2,128)(2,1)S(1)}, bf16[2,2,256,512]{2,1,3,0:T(2,128)(2,1)S(1)}, u32[]{:S(2)}, u32[]{:S(2)}) %collective-permute-start.6) | collective-permute-done | bytes 1048608 | tf_op jit(solution)/shard_map/ppermute | solution.py:20
  283.5 10.8 %collective-permute-done.7 = bf16[2,2,256,512]{2,1,3,0:T(2,128)(2,1)S(1)} collective-permute-done((bf16[2,2,256,512]{2,1,3,0:T(2,128)(2,1)S(1)}, bf16[2,2,256,512]{2,1,3,0:T(2,128)(2,1)S(1)}, u32[]{:S(2)}, u32[]{:S(2)}) %collective-permute-start.7) | collective-permute-done | bytes 1048608 | tf_op jit(solution)/shard_map/ppermute | solution.py:20
  294.2 2.0 broadcast_select_fusion.7
  308.7 2.7 convolution_convert_fusion
  311.4 43.1 %reduce-scatter.2.cloned.1.call-done = bf16[2,256,512]{2,1,0:T(8,128)(2,1)} async-done(((bf16[2,256,2048]{2,1,0:T(8,128)(2,1)}), bf16[2,256,512]{2,1,0:T(8,128)(2,1)}) %reduce-scatter.2.cloned.1.call-update) | async-done | bytes 524304 | tf_op jit(solution)/shard_map/reduce_scatter | solution.py:185
  (192 shorter events, 121.3 us)
Async XLA Ops:
  7.2 1.6 copy-start
  7.2 94.1 %all-reduce.3.cloned.1.call-start = ((), (), s32[]{:S(2)}) async-start(), calls=%async_computation.2 | async-start | bytes 3145728 | tf_op jit(solution)/shard_map/psum | solution.py:107
  22.1 5.0 %copy-start.2 = (bf16[2,256,3,512]{1,0,3,2:T(2,128)(2,1)S(1)}, bf16[2,256,3,512]{1,0,3,2:T(2,128)(2,1)}, u32[]{:S(2)}) copy-start(bf16[2,256,3,512]{1,0,3,2:T(2,128)(2,1)} %reshape.210) | copy-start | bytes 4718596
  26.7 6.8 %copy-start.28 = (bf16[2048,1]{0,1:T(2,128)(2,1)S(1)}, bf16[2048,1]{0,1:T(2,128)(2,1)}, u32[]{:S(2)}) copy-start(bf16[2048,1]{0,1:T(2,128)(2,1)} %param.10) | copy-start | bytes 12292
  26.7 160.8 %collective-permute-start = (bf16[2,2,256,512]{2,1,3,0:T(2,128)(2,1)}, bf16[2,2,256,512]{2,1,3,0:T(2,128)(2,1)}, u32[]{:S(2)}, u32[]{:S(2)}) collective-permute-start(bf16[2,2,256,512]{2,1,3,0:T(2,128)(2,1)} %pad_maximum_fusion), channel_id=1, source_target_pairs={{0,4},{4,8},{8,12},{12,16},{16,20},{20,24},{24,28},{28,0},{1,5},{5... | collective-permute-start | bytes 3145736 | tf_op jit(solution)/shard_map/ppermute | solution.py:20
  31.5 3.5 copy-start.5
  34.1 1.2 copy-start.7
  34.1 1.3 copy-start.24
  39.4 4.9 %copy-start.10 = (f32[1,512,512]{2,1,0:T(8,128)S(1)}, f32[1,512,512]{2,1,0:T(8,128)}, u32[]{:S(2)}) copy-start(f32[1,512,512]{2,1,0:T(8,128)} %param.14) | copy-start | bytes 3145732
  39.4 315.0 %reduce-scatter.2.cloned.1.call-start = ((), (), s32[]{:S(2)}) async-start(), calls=%async_computation.1 | async-start | bytes 2621440 | tf_op jit(solution)/shard_map/reduce_scatter | solution.py:185
  107.0 1.9 copy-start.27
  129.7 2.1 copy-start.25
  129.7 2.1 copy-start.26
  156.5 4.9 %copy-start.3 = (f32[512,512]{1,0:T(8,128)}, f32[512,512]{1,0:T(8,128)S(1)}, u32[]{:S(2)}) copy-start(f32[512,512]{1,0:T(8,128)S(1)} %convolution_add_fusion.6) | copy-start | bytes 3145732
  187.4 2.0 copy-start.8
  187.4 15.5 %collective-permute-start.1 = (bf16[2,2,256,512]{2,1,3,0:T(2,128)(2,1)}, bf16[2,2,256,512]{2,1,3,0:T(2,128)(2,1)}, u32[]{:S(2)}, u32[]{:S(2)}) collective-permute-start(bf16[2,2,256,512]{2,1,3,0:T(2,128)(2,1)} %collective-permute-done), channel_id=1, source_target_pairs={{0,4},{4,8},{8,12},{12,16},{16,20},{20,24},{24,28},{28,0},{1,5},{5... | collective-permute-start | bytes 3145736 | tf_op jit(solution)/shard_map/ppermute | solution.py:20
  189.4 2.0 copy-start.4
  189.4 2.0 copy-start.11
  189.5 2.0 copy-start.15
  191.4 12.6 %copy-start.17 = (f32[512,512]{1,0:T(8,128)}, f32[512,512]{1,0:T(8,128)S(1)}, u32[]{:S(2)}) copy-start(f32[512,512]{1,0:T(8,128)S(1)} %fusion.33) | copy-start | bytes 3145732
  191.4 2.9 copy-start.6
  194.4 8.6 %copy-start.18 = (bf16[1,256,1,512]{3,1,2,0:T(8,128)(2,1)S(1)}, bf16[1,256,1,512]{3,1,2,0:T(8,128)(2,1)}, u32[]{:S(2)}) copy-start(bf16[1,256,1,512]{3,1,2,0:T(8,128)(2,1)} %copy.1241) | copy-start | bytes 786436
  196.3 10.5 %copy-start.16 = (f32[512,512]{1,0:T(8,128)}, f32[512,512]{1,0:T(8,128)S(1)}, u32[]{:S(2)}) copy-start(f32[512,512]{1,0:T(8,128)S(1)} %fusion.31) | copy-start | bytes 3145732
  202.9 15.3 %collective-permute-start.2 = (bf16[2,2,256,512]{2,1,3,0:T(2,128)(2,1)}, bf16[2,2,256,512]{2,1,3,0:T(2,128)(2,1)S(1)}, u32[]{:S(2)}, u32[]{:S(2)}) collective-permute-start(bf16[2,2,256,512]{2,1,3,0:T(2,128)(2,1)} %collective-permute-done.1), channel_id=1, source_target_pairs={{0,4},{4,8},{8,12},{12,16},{16,20},{20,24},{24,28},{28,0},{1,5},{5... | collective-permute-start | bytes 3145736 | tf_op jit(solution)/shard_map/ppermute | solution.py:20
  218.3 15.3 %collective-permute-start.3 = (bf16[2,2,256,512]{2,1,3,0:T(2,128)(2,1)S(1)}, bf16[2,2,256,512]{2,1,3,0:T(2,128)(2,1)S(1)}, u32[]{:S(2)}, u32[]{:S(2)}) collective-permute-start(bf16[2,2,256,512]{2,1,3,0:T(2,128)(2,1)S(1)} %collective-permute-done.2), channel_id=1, source_target_pairs={{0,4},{4,8},{8,12},{12,16},{16,20},{20,24},{24,28},{28,0},{1,5},{5... | collective-permute-start | bytes 3145736 | tf_op jit(solution)/shard_map/ppermute | solution.py:20
  233.5 15.1 %collective-permute-start.4 = (bf16[2,2,256,512]{2,1,3,0:T(2,128)(2,1)S(1)}, bf16[2,2,256,512]{2,1,3,0:T(2,128)(2,1)S(1)}, u32[]{:S(2)}, u32[]{:S(2)}) collective-permute-start(bf16[2,2,256,512]{2,1,3,0:T(2,128)(2,1)S(1)} %collective-permute-done.3), channel_id=1, source_target_pairs={{0,4},{4,8},{8,12},{12,16},{16,20},{20,24},{24,28},{28,0},{1,5},{5... | collective-permute-start | bytes 3145736 | tf_op jit(solution)/shard_map/ppermute | solution.py:20
  248.7 15.1 %collective-permute-start.5 = (bf16[2,2,256,512]{2,1,3,0:T(2,128)(2,1)S(1)}, bf16[2,2,256,512]{2,1,3,0:T(2,128)(2,1)S(1)}, u32[]{:S(2)}, u32[]{:S(2)}) collective-permute-start(bf16[2,2,256,512]{2,1,3,0:T(2,128)(2,1)S(1)} %collective-permute-done.4), channel_id=1, source_target_pairs={{0,4},{4,8},{8,12},{12,16},{16,20},{20,24},{24,28},{28,0},{1,5},{5... | collective-permute-start | bytes 3145736 | tf_op jit(solution)/shard_map/ppermute | solution.py:20
  263.8 15.3 %collective-permute-start.6 = (bf16[2,2,256,512]{2,1,3,0:T(2,128)(2,1)S(1)}, bf16[2,2,256,512]{2,1,3,0:T(2,128)(2,1)S(1)}, u32[]{:S(2)}, u32[]{:S(2)}) collective-permute-start(bf16[2,2,256,512]{2,1,3,0:T(2,128)(2,1)S(1)} %collective-permute-done.5), channel_id=1, source_target_pairs={{0,4},{4,8},{8,12},{12,16},{16,20},{20,24},{24,28},{28,0},{1,5},{5... | collective-permute-start | bytes 3145736 | tf_op jit(solution)/shard_map/ppermute | solution.py:20
  279.1 15.1 %collective-permute-start.7 = (bf16[2,2,256,512]{2,1,3,0:T(2,128)(2,1)S(1)}, bf16[2,2,256,512]{2,1,3,0:T(2,128)(2,1)S(1)}, u32[]{:S(2)}, u32[]{:S(2)}) collective-permute-start(bf16[2,2,256,512]{2,1,3,0:T(2,128)(2,1)S(1)} %collective-permute-done.6), channel_id=1, source_target_pairs={{0,4},{4,8},{8,12},{12,16},{16,20},{20,24},{24,28},{28,0},{1,5},{5... | collective-permute-start | bytes 3145736 | tf_op jit(solution)/shard_map/ppermute | solution.py:20
  306.7 1.9 copy-start.29
  306.7 1.9 copy-start.30
  308.7 45.8 %copy-start.1 = (bf16[2,256,2048]{2,1,0:T(8,128)(2,1)S(1)}, bf16[2,256,2048]{2,1,0:T(8,128)(2,1)}, u32[]{:S(2)}) copy-start(bf16[2,256,2048]{2,1,0:T(8,128)(2,1)} %param.8) | copy-start | bytes 6291460
  (9 other events, 9.6 us)
Sparse Core Ops, SparseCore 0:
  39.6 61.6 all-reduce.2
  311.5 42.9 reduce-scatter.1
where the time goes:
time: 369 us; the launch traced here: 362 us
  waiting for transfers between devices  159 us (43%)
  matrix products  116 us (31%)
  local copies, waits for them, and re-layouts  42.1 us (11%)
  other arithmetic  25.3 us (7%)
  between operations  17.8 us (5%)
    ppermute x8, waiting for transfers between devices, passed_along(): return lax.ppermute(value, axis, pairs)  61.5 us
    psum x1, waiting for transfers between devices, update_weights(): lax.psum(grads[2].astype(jnp.bfloat16), 'ctx').astype(jnp.float32)  54.5 us
    reduce_scatter x1, waiting for transfers between devices, shards(): lax.psum_scatter(terms.astype(jnp.bfloat16), 'head', scatter_dimension=2,...  43.1 us
    dot_general x15, matrix products, gram_of(): lax.dot_general(current, current, (((0,), (0,)), ((), ())), precision=lax...  30.2 us
    dot_general x15, matrix products, ns_update(): jnp.dot(current, poly, precision=lax.Precision.HIGHEST)  29.9 us
    dot_general x15, matrix products, ns_update(): jnp.dot(gram, gram, precision=lax.Precision.HIGHEST)  29.5 us
    select_n x8, other arithmetic, shards(): jnp.where(ctx_index >= distance, piece[:, block_num], piece[:, block_num...  17.7 us
    slice x16, local copies, waits for them, and re-layouts, shards(): key_blocks.append(chosen[0])  16.8 us
  transfers between devices with their start and end apart: 10, of which 9 were waited for; matrix products, arithmetic and copies ran while one was open for 41% of the time, Pallas kernels for 0%

commit v1 on v0

v1 whole, which is shorter than its diff:
```python
import functools

import jax
import jax.numpy as jnp
from jax import lax
from jax.experimental import pallas as pl
from jax.experimental.pallas import tpu as pltpu
from jax.sharding import PartitionSpec as P

WINDOW = 2048
NS_STEPS = 5

coeff_a = 3.4445
coeff_b = -4.775
coeff_c = 2.0315
fast_step = 0.5
norm_eps = 1e-06
BF = jnp.bfloat16
F32 = jnp.float32
VMEM = pl.BlockSpec(memory_space=pltpu.VMEM)
LIMIT = 60 * 1024 * 1024


def mm(left, right, dims):
    return lax.dot_general(left, right, (dims, ((), ())), preferred_element_type=F32)


def nn(left, right):
    return mm(left, right, ((1,), (0,)))


def nt(left, right):
    return mm(left, right, ((1,), (1,)))


def tn(left, right):
    return mm(left, right, ((0,), (0,)))


def project_kernel(rows, tok, w, wr, f1, f3, f2, q_ref, kv_ref, g_ref, kv_s):
    step = pl.program_id(0)
    res = nn(tok[...], w[...]).astype(BF)

    @pl.when(step < 2)
    def _():
        kv_ref[...] = res
        kv_s[step] = res

    @pl.when(step == 2)
    def _():
        q_ref[...] = res
        keys = kv_s[0, :rows]
        vals = kv_s[1, :rows]
        logit = jnp.sum(
            tok[:rows].astype(F32) * wr[...].astype(F32), axis=1, keepdims=True
        )
        rate = jnp.maximum(logit, 0.0) + jnp.log1p(jnp.exp(-jnp.abs(logit)))
        target = (-rate * vals.astype(F32)).astype(BF)
        h1 = nn(keys, f1[...].astype(BF))
        h3 = nn(keys, f3[...].astype(BF))
        sig = jax.nn.sigmoid(h1)
        silu = h1 * sig
        act = (silu * h3).astype(BF)
        dact = nt(target, f2[...].astype(BF))
        d1 = (dact * h3 * (sig * (1.0 + h1 * (1.0 - sig)))).astype(BF)
        d3 = (dact * silu).astype(BF)
        g_ref[0] = tn(keys, d1).astype(BF)
        g_ref[1] = tn(keys, d3).astype(BF)
        g_ref[2] = tn(act, target).astype(BF)


def project(flat, rows, w_qkv, w_rate, f1, f3, f2):
    total, width = flat.shape
    dh = f1.shape[0]
    fh = f1.shape[1]
    whole = lambda *shape: pl.BlockSpec(shape, lambda n: (0,) * len(shape))
    return pl.pallas_call(
        functools.partial(project_kernel, rows),
        grid=(3,),
        in_specs=[
            whole(total, width),
            pl.BlockSpec((width, dh), lambda n: (0, lax.rem(n + 1, 3))),
            whole(1, width),
            whole(dh, fh),
            whole(dh, fh),
            whole(fh, dh),
        ],
        out_specs=[
            whole(total, dh),
            pl.BlockSpec((total, dh), lambda n: (0, jnp.minimum(n, 1))),
            whole(3, dh, fh),
        ],
        out_shape=[
            jax.ShapeDtypeStruct((total, dh), BF),
            jax.ShapeDtypeStruct((total, 2 * dh), BF),
            jax.ShapeDtypeStruct((3, dh, fh), BF),
        ],
        scratch_shapes=[pltpu.VMEM((2, total, dh), BF)],
        compiler_params=pltpu.CompilerParams(vmem_limit_bytes=LIMIT),
        cost_estimate=pl.CostEstimate(
            flops=2 * total * width * 3 * dh, bytes_accessed=2 * width * 3 * dh, transcendentals=0
        ),
        name="project",
    )(flat, w_qkv, w_rate, f1, f3, f2)


def ns_kernel(g_ref, f1, f3, f2, o1, o3, o2, x_ref):
    for i in range(3):
        g = g_ref[i].astype(F32)
        x_ref[i] = g * lax.rsqrt(jnp.sum(g * g) + norm_eps)

    def step(_, carry):
        for i in range(3):
            x = x_ref[i]
            xb = x.astype(BF)
            gram = nt(xb, xb)
            gb = gram.astype(BF)
            poly = coeff_b * gram + coeff_c * nn(gb, gb)
            x_ref[i] = coeff_a * x + nn(poly.astype(BF), xb)
        return carry

    lax.fori_loop(0, NS_STEPS, step, 0)
    for i, (f, o) in enumerate(((f1, o1), (f3, o3), (f2, o2))):
        o[...] = f[...] - fast_step * x_ref[i]


def newton(total, f1, f3, f2):
    shape = f1.shape
    return pl.pallas_call(
        ns_kernel,
        in_specs=[VMEM] * 4,
        out_specs=[VMEM] * 3,
        out_shape=[jax.ShapeDtypeStruct(shape, F32)] * 3,
        scratch_shapes=[pltpu.VMEM((3,) + shape, F32)],
        compiler_params=pltpu.CompilerParams(vmem_limit_bytes=LIMIT // 2),
        cost_estimate=pl.CostEstimate(
            flops=45 * 2 * shape[0] ** 3, bytes_accessed=9 << 20, transcendentals=0
        ),
        name="newton",
    )(total, f1, f3, f2)


def attend_kernel(reach, blocks, n_ctx, q_ref, kv_ref, o_ref, m_s, l_s, acc):
    me = lax.axis_index("ctx")
    rows = q_ref.shape[0] // blocks
    dh = q_ref.shape[1]
    scale = dh ** (-0.5)
    for b in range(blocks):
        here = b * n_ctx + me
        q = q_ref[b * rows : (b + 1) * rows]
        m_s[...] = jnp.full_like(m_s, -1e30)
        l_s[...] = jnp.zeros_like(l_s)
        acc[...] = jnp.zeros_like(acc)

        def piece(s, carry):
            g = here - reach + s
            dev = lax.rem(g, n_ctx)
            at = pl.multiple_of(lax.div(g, n_ctx) * rows, rows)
            k = kv_ref[dev, pl.ds(at, rows), :dh]
            v = kv_ref[dev, pl.ds(at, rows), dh:]
            sc = nt(q, k) * scale
            diff = lax.broadcasted_iota(jnp.int32, (rows, rows), 0) - lax.broadcasted_iota(
                jnp.int32, (rows, rows), 1
            )
            off = diff + (reach - s) * rows
            sc = jnp.where((off >= 0) & (off < WINDOW), sc, -1e30)
            old = m_s[...]
            new = jnp.maximum(old, jnp.max(sc, axis=1, keepdims=True))
            p = jnp.where(sc > -1e29, jnp.exp(sc - new), 0.0)
            fade = jnp.exp(old - new)
            l_s[...] = l_s[...] * fade + jnp.sum(p, axis=1, keepdims=True)
            acc[...] = acc[...] * fade + nn(p.astype(BF), v)
            m_s[...] = new
            return carry

        lax.fori_loop(jnp.maximum(reach - here, 0), reach + 1, piece, 0)
        o_ref[b * rows : (b + 1) * rows] = acc[...] / l_s[...]


def attend(q, kv, blocks, n_ctx):
    rows = q.shape[0] // blocks
    dh = q.shape[1]
    reach = WINDOW // rows
    return pl.pallas_call(
        functools.partial(attend_kernel, reach, blocks, n_ctx),
        in_specs=[VMEM] * 2,
        out_specs=VMEM,
        out_shape=jax.ShapeDtypeStruct(q.shape, F32),
        scratch_shapes=[
            pltpu.VMEM((rows, 1), F32),
            pltpu.VMEM((rows, 1), F32),
            pltpu.VMEM((rows, dh), F32),
        ],
        compiler_params=pltpu.CompilerParams(vmem_limit_bytes=LIMIT),
        cost_estimate=pl.CostEstimate(
            flops=4 * q.shape[0] * dh * (WINDOW + rows),
            bytes_accessed=q.shape[0] * dh * 2 * 20,
            transcendentals=0,
        ),
        name="attend",
    )(q, kv)


def finish_kernel(q_ref, at_ref, f1, f3, f2, gain, wo, o_ref):
    q = q_ref[...]
    h1 = nn(q, f1[...].astype(BF))
    h3 = nn(q, f3[...].astype(BF))
    act = (jax.nn.silu(h1) * h3).astype(BF)
    out = nn(act, f2[...].astype(BF))
    inv = lax.rsqrt(jnp.mean(out * out, axis=1, keepdims=True) + norm_eps)
    both = (at_ref[...] + out * inv * gain[...]).astype(BF)
    o_ref[...] = nn(both, wo[...]).astype(BF)


def finish(q, att, f1, f3, f2, gain, wo):
    return pl.pallas_call(
        finish_kernel,
        in_specs=[VMEM] * 7,
        out_specs=VMEM,
        out_shape=jax.ShapeDtypeStruct((q.shape[0], wo.shape[1]), BF),
        compiler_params=pltpu.CompilerParams(vmem_limit_bytes=LIMIT // 2),
        cost_estimate=pl.CostEstimate(
            flops=2 * q.shape[0] * wo.shape[0] * (wo.shape[1] + 1536),
            bytes_accessed=6 << 20,
            transcendentals=0,
        ),
        name="finish",
    )(q, att, f1, f3, f2, gain, wo)


def shards(tokens, w_qkv, w_rate, w_out, fw_gain, fast_first, fast_third, fast_second):
    blocks, rows, width = tokens.shape
    dh = w_out.shape[1]
    n_ctx = lax.axis_size("ctx")
    flat = tokens.reshape(blocks * rows, width)
    fast = (fast_first[0], fast_third[0], fast_second[0])
    q, kv, grads = project(
        flat, rows, w_qkv.reshape(width, 3 * dh), w_rate.reshape(1, width), *fast
    )
    total = lax.psum(grads, "ctx")
    every = lax.all_gather(kv, "ctx")
    att = attend(q, every, blocks, n_ctx)
    current = fast
    mixed = []
    for b in range(blocks):
        part = slice(b * rows, (b + 1) * rows)
        terms = finish(q[part], att[part], *current, fw_gain, w_out[0])
        mixed.append(lax.psum_scatter(terms, "head", scatter_dimension=1, tiled=True))
        if b + 1 < blocks:
            current = newton(total, *current)
    return (jnp.stack(mixed),) + tuple(f[None] for f in current)


def solution(mesh):
    placed = (
        P(None, "ctx", None),
        P(None, "head", None),
        P(None, "head"),
        P("head", None, None),
        P("head", None),
        P("head", None, None),
        P("head", None, None),
        P("head", None, None),
    )
    return jax.shard_map(
        shards,
        mesh=mesh,
        in_specs=placed,
        out_specs=(
            P(None, "ctx", "head"),
            P("head", None, None),
            P("head", None, None),
            P("head", None, None),
        ),
        check_vma=False,
    )
```

time: 369 us -> 203 us (0.55); the launches traced: 362 us -> 202 us
  matrix products: 116 us -> 0 us
  Pallas kernels: 0 us -> 44.5 us
  waiting for transfers between devices: 159 us -> 127 us
  local copies, waits for them, and re-layouts: 42.1 us -> 14.7 us
  other arithmetic: 25.3 us -> 1.87 us
  between operations: 17.8 us -> 13.8 us
    dot_general x62 -> x0, matrix products: 116 us -> none  [the longest x15 30.2 us: gram_of(): lax.dot_general(current, current, (((0,), (0,)), ((), ())), precision=lax...]
    ppermute x8 -> x0, waiting for transfers between devices: 61.5 us -> none  [passed_along(): return lax.ppermute(value, axis, pairs)]
    all_gather x0 -> x1, waiting for transfers between devices: none -> 56.1 us  [shards(): every = lax.all_gather(kv, 'ctx')]
    pallas_call x0 -> x5, Pallas kernels: none -> 44.5 us  [the longest x1 16.9 us: newton(): pl.pallas_call(ns_kernel, in_specs=[VMEM] * 4, out_specs=[VMEM] * 3, out_...]
    slice x20 -> x2, local copies, waits for them, and re-layouts: 24.6 us -> 1.48 us  [shards(): terms = finish(q[part], att[part], *current, fw_gain, w_out[0])]
    select_n x9 -> x0, other arithmetic: 17.7 us -> none  [the longest x8 17.7 us: shards(): jnp.where(ctx_index >= distance, piece[:, block_num], piece[:, block_num...]
    reduce_scatter x1 -> x2, waiting for transfers between devices: 43.1 us -> 28.9 us  [shards(): lax.psum_scatter(terms, 'head', scatter_dimension=1, tiled=True)]
    psum x1, waiting for transfers between devices: 54.5 us -> 41.6 us  [shards(): total = lax.psum(grads, 'ctx')]
  transfers between devices with their start and end apart: 10 -> 4, of which waited for: 9 -> 4; matrix products, arithmetic and copies ran while one was open for 41% -> 1% of each run, Pallas kernels for 0% -> 17%
where the time goes in v1:
time: 203 us; the launch traced here: 202 us
  waiting for transfers between devices  127 us (63%)
  Pallas kernels  44.5 us (22%)
  local copies, waits for them, and re-layouts  14.7 us (7%)
  between operations  13.8 us (7%)
    all_gather x1, waiting for transfers between devices, shards(): every = lax.all_gather(kv, 'ctx')  56.1 us
    psum x1, waiting for transfers between devices, shards(): total = lax.psum(grads, 'ctx')  41.6 us
    reduce_scatter x2, waiting for transfers between devices, shards(): lax.psum_scatter(terms, 'head', scatter_dimension=1, tiled=True)  28.9 us
    pallas_call x1, Pallas kernels, newton(): pl.pallas_call(ns_kernel, in_specs=[VMEM] * 4, out_specs=[VMEM] * 3, out_...  16.9 us
    unnamed x26, local copies, waits for them, and re-layouts  13.2 us
    pallas_call x1, Pallas kernels, attend(): pl.pallas_call(functools.partial(attend_kernel, reach, blocks, n_ctx), in...  12.4 us
    pallas_call x1, Pallas kernels, project(): pl.pallas_call(functools.partial(project_kernel, rows), grid=(3,), in_spe...  10.6 us
    pallas_call x2, Pallas kernels, finish(): pl.pallas_call(finish_kernel, in_specs=[VMEM] * 7, out_specs=VMEM, out_sh...  4.73 us
  transfers between devices with their start and end apart: 4, of which 4 were waited for; matrix products, arithmetic and copies ran while one was open for 1% of the time, Pallas kernels for 17%

profile of v1, /device:TPU:0, one launch (start us, length us, event | category | flops | bytes accessed | tf_op | source)
XLA Modules:
  0.0 202.3 jit_solution(4972423685395285404)
XLA Ops:
  7.2 0.0 all-gather.3.cloned.1.call-start
  7.2 10.6 %project.1 = (bf16[512,512]{1,0:T(8,128)(2,1)}, bf16[512,1024]{1,0:T(8,128)(2,1)}, bf16[3,512,512]{2,1,0:T(8,128)(2,1)}) custom-call(bf16[512,2048]{1,0:T(8,128)(2,1)} %bitcast.31, bf16[2048,1536]{1,0:T(8,128)(2,1)} %bitcast.30, bf16[1,2048]{1,0:T(2,128)(2,1)} %bitcast.32, f32[512,512]{1,0:T(8,128)} %bitcast.15, f32[512,512]{1,0:T(8,128)} %bitcast.18, ...), custom_call_target="tpu_custom_call" | custom-call | flops 3221225472 | bytes 6291456 | tf_op jit(solution)/shard_map/project/pallas_call | solution.py:77
  17.8 0.0 all-gather.3.cloned.1.call-update
  17.8 0.0 all-reduce.2.cloned.1.call-start
  17.9 0.7 all-reduce.2.cloned.1.call-update
  18.6 0.0 reduce-scatter.3.cloned.1.call-start
  18.6 0.2 copy-done.12
  18.9 56.1 %all-gather.3.cloned.1.call-done = bf16[4096,1024]{1,0:T(8,128)(2,1)} async-done(((bf16[512,1024]{1,0:T(8,128)(2,1)}), bf16[4096,1024]{1,0:T(8,128)(2,1)}) %all-gather.3.cloned.1.call-update) | async-done | bytes 8388624 | tf_op jit(solution)/shard_map/all_gather | solution.py:241
  74.9 12.4 %attend.1 = f32[512,512]{1,0:T(8,128)} custom-call(bf16[512,512]{1,0:T(8,128)(2,1)} %get-tuple-element.10.q_ref, bf16[8,512,1024]{2,1,0:T(8,128)(2,1)} %bitcast.27), custom_call_target="tpu_custom_call" | custom-call | flops 2415919104 | bytes 10485760 | tf_op jit(solution)/shard_map/attend/pallas_call | solution.py:184
  87.3 1.4 fusion
  88.7 0.5 copy-done
  89.3 0.0 copy-done.10
  89.3 1.2 copy-done.1
  90.5 1.2 copy-done.3
  91.7 1.2 copy-done.5
  93.0 2.4 %finish.2 = bf16[256,2048]{1,0:T(8,128)(2,1)} custom-call(bf16[256,512]{1,0:T(8,128)(2,1)S(1)} %get-tuple-element.18.q_ref, f32[256,512]{1,0:T(8,128)S(1)} %get-tuple-element.16.at_ref, f32[512,512]{1,0:T(8,128)S(1)} %bitcast.16, f32[512,512]{1,0:T(8,128)S(1)} %bitcast.19, f32[512,512]{1,0:T(8,128)S(1)} %bitcast.22, f32[1,512]{1,0:T(1,128)S(1)} %copy-done.10, ...), custom_call_target="tpu_custom_call" | custom-call | flops 939524096 | bytes 6291456 | tf_op jit(solution)/shard_map/finish/pallas_call | solution.py:216
  95.4 0.0 reduce-scatter.3.cloned.1.call-update
  95.4 0.0 reduce-scatter.5.cloned.1.call-start
  95.4 41.6 %all-reduce.2.cloned.1.call-done.g_ref = bf16[3,512,512]{2,1,0:T(8,128)(2,1)} async-done(((bf16[3,512,512]{2,1,0:T(8,128)(2,1)}), bf16[3,512,512]{2,1,0:T(8,128)(2,1)}) %all-reduce.2.cloned.1.call-update) | async-done | bytes 1572880 | tf_op jit(solution)/shard_map/psum | solution.py:240
  137.0 1.2 copy-done.2
  138.2 1.2 copy-done.4
  139.4 1.2 copy-done.6
  140.7 1.4 copy-done.11
  142.1 16.9 %newton.1 = (f32[512,512]{1,0:T(8,128)}, f32[512,512]{1,0:T(8,128)}, f32[512,512]{1,0:T(8,128)}) custom-call(bf16[3,512,512]{2,1,0:T(8,128)(2,1)S(1)} %copy-done.11, f32[512,512]{1,0:T(8,128)S(1)} %bitcast.17, f32[512,512]{1,0:T(8,128)S(1)} %bitcast.20, f32[512,512]{1,0:T(8,128)S(1)} %bitcast.23), custom_call_target="tpu_custom_call" | custom-call | flops 12079595520 | bytes 9437184 | tf_op jit(solution)/shard_map/newton/pallas_call | solution.py:129
  158.9 1.2 copy-done.7
  160.1 1.2 copy-done.8
  161.4 1.2 copy-done.9
  162.6 2.4 %finish.3 = bf16[256,2048]{1,0:T(8,128)(2,1)} custom-call(bf16[256,512]{1,0:T(8,128)(2,1)S(1)} %get-tuple-element.19.q_ref, f32[256,512]{1,0:T(8,128)S(1)} %get-tuple-element.17.at_ref, f32[512,512]{1,0:T(8,128)S(1)} %copy-done.7, f32[512,512]{1,0:T(8,128)S(1)} %copy-done.8, f32[512,512]{1,0:T(8,128)S(1)} %copy-done.9, f32[1,512]{1,0:T(1,128)S(1)} %copy-done.10, ...), custom_call_target="tpu_custom_call" | custom-call | flops 939524096 | bytes 6291456 | tf_op jit(solution)/shard_map/finish/pallas_call | solution.py:216
  165.0 0.0 reduce-scatter.5.cloned.1.call-update
  165.0 0.9 reduce-scatter.3.cloned.1.call-done
  165.9 28.0 %reduce-scatter.5.cloned.1.call-done = bf16[256,512]{1,0:T(8,128)(2,1)} async-done(((bf16[256,2048]{1,0:T(8,128)(2,1)}), bf16[256,512]{1,0:T(8,128)(2,1)}) %reduce-scatter.5.cloned.1.call-update) | async-done | bytes 262160 | tf_op jit(solution)/shard_map/reduce_scatter | solution.py:248
  193.9 1.9 pad_maximum_fusion
  (14 shorter events, 0.1 us)
Async XLA Ops:
  7.2 67.8 %all-gather.3.cloned.1.call-start = ((), (), s32[]{:S(2)}) async-start(), calls=%async_computation.5 | async-start | bytes 9437184 | tf_op jit(solution)/shard_map/all_gather | solution.py:241
  17.8 1.0 copy-start.12
  17.8 119.2 %all-reduce.2.cloned.1.call-start = ((), (), s32[]{:S(2)}) async-start(), calls=%async_computation.3 | async-start | bytes 3145728 | tf_op jit(solution)/shard_map/psum | solution.py:240
  18.6 147.4 %reduce-scatter.3.cloned.1.call-start = ((), (), s32[]{:S(2)}) async-start(), calls=%async_computation.2 | async-start | bytes 1310720 | tf_op jit(solution)/shard_map/reduce_scatter | solution.py:248
  87.3 2.0 copy-start
  87.3 2.0 copy-start.10
  89.3 1.2 copy-start.1
  90.5 1.2 copy-start.3
  91.7 1.2 copy-start.5
  95.4 98.5 %reduce-scatter.5.cloned.1.call-start = ((), (), s32[]{:S(2)}) async-start(), calls=%async_computation.4 | async-start | bytes 1310720 | tf_op jit(solution)/shard_map/reduce_scatter | solution.py:248
  137.0 1.2 copy-start.2
  138.2 1.2 copy-start.4
  139.4 1.2 copy-start.6
  140.7 1.4 copy-start.11
  158.9 1.2 copy-start.7
  160.1 1.2 copy-start.8
  161.4 1.2 copy-start.9
Sparse Core Ops, SparseCore 0:
  17.9 56.9 all-gather.2
  78.2 58.7 all-reduce.1
  139.3 26.6 reduce-scatter.2
  168.1 25.7 reduce-scatter.4

commit v2 on v1

v2 whole, which is shorter than its diff:
```python
import functools

import jax
import jax.numpy as jnp
from jax import lax
from jax.experimental import pallas as pl
from jax.experimental.pallas import tpu as pltpu
from jax.sharding import PartitionSpec as P

WINDOW = 2048
NS_STEPS = 5

coeff_a = 3.4445
coeff_b = -4.775
coeff_c = 2.0315
fast_step = 0.5
norm_eps = 1e-06
BF = jnp.bfloat16
F32 = jnp.float32
VMEM = pl.BlockSpec(memory_space=pltpu.VMEM)
LIMIT = 60 * 1024 * 1024


def mm(left, right, dims):
    return lax.dot_general(left, right, (dims, ((), ())), preferred_element_type=F32)


def nn(left, right):
    return mm(left, right, ((1,), (0,)))


def nt(left, right):
    return mm(left, right, ((1,), (1,)))


def tn(left, right):
    return mm(left, right, ((0,), (0,)))


def project_kernel(rows, tok, w, wr, f1, f3, f2, q_ref, kv_ref, g_ref, kv_s):
    step = pl.program_id(0)
    res = nn(tok[...], w[...]).astype(BF)

    @pl.when(step < 2)
    def _():
        kv_ref[...] = res
        kv_s[step] = res

    @pl.when(step == 2)
    def _():
        q_ref[...] = res
        keys = kv_s[0, :rows]
        vals = kv_s[1, :rows]
        logit = jnp.sum(
            tok[:rows].astype(F32) * wr[...].astype(F32), axis=1, keepdims=True
        )
        rate = jnp.maximum(logit, 0.0) + jnp.log1p(jnp.exp(-jnp.abs(logit)))
        target = (-rate * vals.astype(F32)).astype(BF)
        h1 = nn(keys, f1[...].astype(BF))
        h3 = nn(keys, f3[...].astype(BF))
        sig = jax.nn.sigmoid(h1)
        silu = h1 * sig
        act = (silu * h3).astype(BF)
        dact = nt(target, f2[...].astype(BF))
        d1 = (dact * h3 * (sig * (1.0 + h1 * (1.0 - sig)))).astype(BF)
        d3 = (dact * silu).astype(BF)
        g_ref[0] = tn(keys, d1).astype(BF)
        g_ref[1] = tn(keys, d3).astype(BF)
        g_ref[2] = tn(act, target).astype(BF)


def project(flat, rows, w_qkv, w_rate, f1, f3, f2):
    total, width = flat.shape
    dh = f1.shape[0]
    fh = f1.shape[1]
    whole = lambda *shape: pl.BlockSpec(shape, lambda n: (0,) * len(shape))
    return pl.pallas_call(
        functools.partial(project_kernel, rows),
        grid=(3,),
        in_specs=[
            whole(total, width),
            pl.BlockSpec((width, dh), lambda n: (0, lax.rem(n + 1, 3))),
            whole(1, width),
            whole(dh, fh),
            whole(dh, fh),
            whole(fh, dh),
        ],
        out_specs=[
            whole(total, dh),
            pl.BlockSpec((total, dh), lambda n: (0, jnp.minimum(n, 1))),
            whole(3, dh, fh),
        ],
        out_shape=[
            jax.ShapeDtypeStruct((total, dh), BF),
            jax.ShapeDtypeStruct((total, 2 * dh), BF),
            jax.ShapeDtypeStruct((3, dh, fh), BF),
        ],
        scratch_shapes=[pltpu.VMEM((2, total, dh), BF)],
        compiler_params=pltpu.CompilerParams(vmem_limit_bytes=LIMIT),
        cost_estimate=pl.CostEstimate(
            flops=2 * total * width * 3 * dh, bytes_accessed=2 * width * 3 * dh, transcendentals=0
        ),
        name="project",
    )(flat, w_qkv, w_rate, f1, f3, f2)


def cross_bits(n, sub):
    bits = [1 << i for i in range(1, n.bit_length() - 1)]
    return bits if sub == 0 else bits[::-1]


def remote(src, dst, send, recv, axis, peer):
    return pltpu.make_async_remote_copy(
        src_ref=src,
        dst_ref=dst,
        send_sem=send,
        recv_sem=recv,
        device_id={axis: peer},
        device_id_type=pl.DeviceIdType.MESH,
    )


def mix_kernel(
    n, nh, blocks, q_ref, kv_ref, g_ref, f1, f3, f2, gain, wo,
    mixed, o1, o3, o2,
    every, half_in, sums, sum_in, total, m_s, l_s, acc, t_buf, t_in,
    h_send, h_recv, d_send, d_recv, a_send, a_recv, k_send, k_recv, r_send, r_recv,
):
    me = lax.axis_index("ctx")
    hme = lax.axis_index("head")
    rows = q_ref.shape[0] // blocks
    dh = q_ref.shape[1]
    reach = WINDOW // rows
    scale = dh ** (-0.5)
    cols = wo.shape[1] // nh
    half = g_ref.shape[1] // 2
    quarter = half // 2
    piece_rows = rows // 2
    core = lax.rem(me, 2)
    mine = pl.multiple_of(core * half, half)
    theirs = pl.multiple_of((1 - core) * half, half)
    levels = n.bit_length() - 2

    barrier = pltpu.get_barrier_semaphore()
    ctx_bits = [1 << i for i in range(n.bit_length() - 1)]
    for bit in ctx_bits:
        pl.semaphore_signal(
            barrier, inc=1, device_id={"ctx": me ^ bit}, device_id_type=pl.DeviceIdType.MESH
        )
    for r in range(1, nh):
        pl.semaphore_signal(
            barrier,
            inc=1,
            device_id={"head": lax.rem(hme + r, nh)},
            device_id_type=pl.DeviceIdType.MESH,
        )
    pl.semaphore_wait(barrier, len(ctx_bits) + nh - 1)

    started = []

    def go(copy):
        copy.start()
        started.append(copy)

    def place(p):
        return pl.ds((p // 2) * rows + (p % 2) * piece_rows, piece_rows)

    def kv_copy(p, c, bit):
        dst = every.at[me ^ c, place(p)]
        src = kv_ref.at[place(p)] if c == 0 else dst
        return remote(
            src, dst, k_send.at[p, c | bit], k_recv.at[p, c | bit], "ctx", me ^ bit
        )

    def kv_wait(p, c):
        dst = every.at[me ^ c, place(p)]
        bit = c & -c
        remote(dst, dst, k_send.at[p, c], k_recv.at[p, c], "ctx", me ^ bit).wait_recv()

    def later(p, c):
        order = cross_bits(n, p % 2)
        last = max([i for i, bit in enumerate(order) if c & bit], default=-1)
        return order[last + 1 :]

    def pass_on(p, c):
        for bit in later(p, c):
            go(kv_copy(p, c, bit))
        go(kv_copy(p, c, 1))

    def first_hop(p):
        return cross_bits(n, p % 2)[0]

    def part(u):
        return pl.ds(u * quarter, quarter)

    def sum_copy(t, u):
        return remote(
            sums.at[t, :, part(u)],
            sum_in.at[t, :, part(u)],
            a_send.at[t, u],
            a_recv.at[t, u],
            "ctx",
            me ^ cross_bits(n, u)[t],
        )

    first = remote(g_ref.at[:, pl.ds(theirs, half)], half_in, h_send, h_recv, "ctx", me ^ 1)
    go(first)
    every[me] = kv_ref[...]
    first.wait_recv()
    sums[0] = (g_ref[:, pl.ds(mine, half)].astype(F32) + half_in[...].astype(F32)).astype(BF)
    for t in range(levels):
        step = [sum_copy(t, u) for u in range(2)]
        for copy in step:
            go(copy)
        if t == levels - 1:
            for p in range(2):
                for bit in cross_bits(n, p):
                    go(kv_copy(p, 0, bit))
            for p in range(2 * blocks):
                go(kv_copy(p, 0, 1))
        for copy in step:
            copy.wait_recv()
        added = (sums[t].astype(F32) + sum_in[t].astype(F32)).astype(BF)
        if t < levels - 1:
            sums[t + 1] = added
        else:
            total[:, pl.ds(mine, half)] = added
    done = total.at[:, pl.ds(mine, half)]
    give = remote(done, done, d_send, d_recv, "ctx", me ^ 1)
    go(give)
    other = total.at[:, pl.ds(theirs, half)]
    remote(other, other, d_send, d_recv, "ctx", me ^ 1).wait_recv()

    for i, x_ref in enumerate((o1, o3, o2)):
        g = total[i].astype(F32)
        x_ref[...] = g * lax.rsqrt(jnp.sum(g * g) + norm_eps)

    def ns_step(_, carry):
        for x_ref in (o1, o3, o2):
            x = x_ref[...]
            xb = x.astype(BF)
            gram = nt(xb, xb)
            gb = gram.astype(BF)
            poly = coeff_b * gram + coeff_c * nn(gb, gb)
            x_ref[...] = coeff_a * x + nn(poly.astype(BF), xb)
        return carry

    early = 3
    lax.fori_loop(0, early, ns_step, 0)
    for p in range(2):
        kv_wait(p, first_hop(p))
        pass_on(p, first_hop(p))
    for p in range(2, 2 * blocks):
        for bit in cross_bits(n, p % 2):
            go(kv_copy(p, 0, bit))
    lax.fori_loop(early, NS_STEPS, ns_step, 0)
    for f, o in ((f1, o1), (f3, o3), (f2, o2)):
        o[...] = f[...] - fast_step * o[...]

    def gather_rest(b):
        pieces = (2 * b, 2 * b + 1)
        evens = sorted(range(2, n, 2), key=lambda c: (bin(c).count("1"), c))
        for c in evens:
            for p in pieces:
                if c != first_hop(p):
                    kv_wait(p, c)
                    pass_on(p, c)
        for c in range(1, n, 2):
            for p in pieces:
                kv_wait(p, c)

    def clear():
        m_s[...] = jnp.full_like(m_s, -1e30)
        l_s[...] = jnp.zeros_like(l_s)
        acc[...] = jnp.zeros_like(acc)

    def attend(b, side):
        here = b * n + me
        q = q_ref[b * rows : (b + 1) * rows]

        def piece(g, carry):
            dev = g - side * n
            k = every[dev, side * rows : (side + 1) * rows, :dh]
            v = every[dev, side * rows : (side + 1) * rows, dh:]
            sc = nt(q, k) * scale
            diff = lax.broadcasted_iota(jnp.int32, (rows, rows), 0) - lax.broadcasted_iota(
                jnp.int32, (rows, rows), 1
            )
            off = diff + (here - g) * rows
            sc = jnp.where((off >= 0) & (off < WINDOW), sc, -1e30)
            old = m_s[...]
            new = jnp.maximum(old, jnp.max(sc, axis=1, keepdims=True))
            p = jnp.where(sc > -1e29, jnp.exp(sc - new), 0.0)
            fade = jnp.exp(old - new)
            l_s[...] = l_s[...] * fade + jnp.sum(p, axis=1, keepdims=True)
            acc[...] = acc[...] * fade + nn(p.astype(BF), v)
            m_s[...] = new
            return carry

        low = jnp.maximum(here - reach, side * n)
        high = jnp.minimum(here, side * n + n - 1)
        lax.fori_loop(low, high + 1, piece, 0)

    def head_copy(b, r):
        peer = lax.rem(hme + r, nh)
        return remote(
            t_buf.at[b, peer],
            t_in.at[b, r - 1],
            r_send.at[b, r - 1],
            r_recv.at[b, r - 1],
            "head",
            peer,
        )

    def finish(b, w1, w3, w2):
        q = q_ref[b * rows : (b + 1) * rows]
        h1 = nn(q, w1[...].astype(BF))
        h3 = nn(q, w3[...].astype(BF))
        act = (jax.nn.silu(h1) * h3).astype(BF)
        out = nn(act, w2[...].astype(BF))
        inv = lax.rsqrt(jnp.mean(out * out, axis=1, keepdims=True) + norm_eps)
        both = (acc[...] / l_s[...] + out * inv * gain[...]).astype(BF)
        for h in range(nh):
            t_buf[b, h] = nn(both, wo[:, h * cols : (h + 1) * cols]).astype(BF)
        copies = [head_copy(b, r) for r in range(1, nh)]
        for copy in copies:
            go(copy)
        return copies

    head_copies = []
    for b in range(blocks):
        clear()
        if b > 0:
            for p in (2 * b, 2 * b + 1):
                kv_wait(p, first_hop(p))
                pass_on(p, first_hop(p))
            attend(b, b - 1)
        gather_rest(b)
        attend(b, b)
        head_copies.append(finish(b, *((f1, f3, f2) if b == 0 else (o1, o3, o2))))
    for b in range(blocks):
        for copy in head_copies[b]:
            copy.wait_recv()
        result = t_buf[b, hme].astype(F32)
        for r in range(nh - 1):
            result = result + t_in[b, r].astype(F32)
        mixed[b] = result.astype(BF)
    for copy in started:
        copy.wait_send()


def mix(n, nh, blocks, q, kv, grads, f1, f3, f2, gain, wo):
    rows = q.shape[0] // blocks
    dh, fh = f1.shape
    cols = wo.shape[1] // nh
    levels = n.bit_length() - 2
    dma = pltpu.SemaphoreType.DMA
    return pl.pallas_call(
        functools.partial(mix_kernel, n, nh, blocks),
        in_specs=[VMEM] * 8,
        out_specs=[VMEM] * 4,
        out_shape=[jax.ShapeDtypeStruct((blocks, rows, cols), BF)]
        + [jax.ShapeDtypeStruct(f.shape, F32) for f in (f1, f3, f2)],
        scratch_shapes=[
            pltpu.VMEM((n,) + kv.shape, BF),
            pltpu.VMEM((3, dh // 2, fh), BF),
            pltpu.VMEM((levels, 3, dh // 2, fh), BF),
            pltpu.VMEM((levels, 3, dh // 2, fh), BF),
            pltpu.VMEM((3, dh, fh), BF),
            pltpu.VMEM((rows, 1), F32),
            pltpu.VMEM((rows, 1), F32),
            pltpu.VMEM((rows, dh), F32),
            pltpu.VMEM((blocks, nh, rows, cols), BF),
            pltpu.VMEM((blocks, nh - 1, rows, cols), BF),
            dma,
            dma,
            dma,
            dma,
            dma((levels, 2)),
            dma((levels, 2)),
            dma((2 * blocks, n)),
            dma((2 * blocks, n)),
            dma((blocks, nh - 1)),
            dma((blocks, nh - 1)),
        ],
        compiler_params=pltpu.CompilerParams(
            vmem_limit_bytes=63 * 1024 * 1024, collective_id=0, has_side_effects=True
        ),
        name="mix",
    )(q, kv, grads, f1, f3, f2, gain, wo)


def shards(tokens, w_qkv, w_rate, w_out, fw_gain, fast_first, fast_third, fast_second):
    blocks, rows, width = tokens.shape
    dh = w_out.shape[1]
    n_ctx = lax.axis_size("ctx")
    flat = tokens.reshape(blocks * rows, width)
    fast = (fast_first[0], fast_third[0], fast_second[0])
    q, kv, grads = project(
        flat, rows, w_qkv.reshape(width, 3 * dh), w_rate.reshape(1, width), *fast
    )
    mixed, *current = mix(
        n_ctx, lax.axis_size("head"), blocks, q, kv, grads, *fast, fw_gain, w_out[0]
    )
    return (mixed,) + tuple(f[None] for f in current)


def solution(mesh):
    placed = (
        P(None, "ctx", None),
        P(None, "head", None),
        P(None, "head"),
        P("head", None, None),
        P("head", None),
        P("head", None, None),
        P("head", None, None),
        P("head", None, None),
    )
    return jax.shard_map(
        shards,
        mesh=mesh,
        in_specs=placed,
        out_specs=(
            P(None, "ctx", "head"),
            P("head", None, None),
            P("head", None, None),
            P("head", None, None),
        ),
        check_vma=False,
    )
```

time: 203 us -> 123 us (0.61)
  the two profiles are of different devices: /device:TPU:0 before, /device:TPU:14 now
where the time goes in v2:
time: 123 us
  Pallas kernels  116 us (94%)
  local copies, waits for them, and re-layouts  6.25 us (5%)
    pallas_call x1, Pallas kernels, mix(): pl.pallas_call(functools.partial(mix_kernel, n, nh, blocks), in_specs=[VM...  106 us
    pallas_call x1, Pallas kernels, project(): pl.pallas_call(functools.partial(project_kernel, rows), grid=(3,), in_spe...  10.5 us
    unnamed x8, local copies, waits for them, and re-layouts  6.25 us

profile of v2, /device:TPU:14, one launch (start us, length us, event | category | flops | bytes accessed | tf_op | source)
XLA Modules:
  0.0 123.0 jit_solution(933908815258900187)
XLA Ops:
  0.6 10.5 %project.1 = (bf16[512,512]{1,0:T(8,128)(2,1)}, bf16[512,1024]{1,0:T(8,128)(2,1)}, bf16[3,512,512]{2,1,0:T(8,128)(2,1)}) custom-call(bf16[512,2048]{1,0:T(8,128)(2,1)} %bitcast.21, bf16[2048,1536]{1,0:T(8,128)(2,1)} %bitcast.20, bf16[1,2048]{1,0:T(2,128)(2,1)} %bitcast.22, f32[512,512]{1,0:T(8,128)} %bitcast.11, f32[512,512]{1,0:T(8,128)} %bitcast.13, ...), custom_call_target="tpu_custom_call" | custom-call | flops 3221225472 | bytes 6291456 | tf_op jit(solution)/shard_map/project/pallas_call | solution.py:77
  11.1 105.6 %mix.1 = (bf16[2,256,512]{2,1,0:T(8,128)(2,1)}, f32[512,512]{1,0:T(8,128)}, f32[512,512]{1,0:T(8,128)}, f32[512,512]{1,0:T(8,128)}) custom-call(bf16[512,512]{1,0:T(8,128)(2,1)} %get-tuple-element.11.q_ref, bf16[512,1024]{1,0:T(8,128)(2,1)} %get-tuple-element.12.kv_ref, bf16[3,512,512]{2,1,0:T(8,128)(2,1)} %get-tuple-element.13.g_ref, f32[512,512]{1,0:T(8,128)} %bitcast.12, ...), custom_call_target="tpu_custom_call" | custom-call | tf_op jit(solution)/shard_map/mix/pallas_call | solution.py:358
  116.8 0.0 copy-start.1
  116.8 2.0 %copy.16 = bf16[2,256,512]{2,1,0:T(8,128)(2,1)} copy(bf16[2,256,512]{2,1,0:T(8,128)(2,1)} %get-tuple-element.22) | data formatting | bytes 1048576
  118.7 0.0 copy-start
  118.7 2.4 %copy.17 = f32[1,512,512]{2,1,0:T(8,128)} copy(f32[1,512,512]{2,1,0:T(8,128)} %bitcast.19) | data formatting | bytes 2097152
  121.1 0.0 copy-done.1
  121.1 1.0 copy.18
  122.0 0.0 copy-done
  122.0 1.0 copy.19
Async XLA Ops:
  116.8 4.3 %copy-start.1 = (f32[512,512]{1,0:T(8,128)S(1)}, f32[512,512]{1,0:T(8,128)}, u32[]{:S(2)}) copy-start(f32[512,512]{1,0:T(8,128)} %get-tuple-element.16) | copy-start | bytes 3145732
  118.7 3.3 %copy-start = (f32[512,512]{1,0:T(8,128)S(1)}, f32[512,512]{1,0:T(8,128)}, u32[]{:S(2)}) copy-start(f32[512,512]{1,0:T(8,128)} %get-tuple-element.17) | copy-start | bytes 3145732

commit v3 on v2

--- a/solution.py
+++ b/solution.py
@@ -257,24 +257,33 @@
     for f, o in ((f1, o1), (f3, o3), (f2, o2)):
         o[...] = f[...] - fast_step * o[...]
 
-    def gather_rest(b):
+    def gather_attend(b):
         pieces = (2 * b, 2 * b + 1)
-        evens = sorted(range(2, n, 2), key=lambda c: (bin(c).count("1"), c))
-        for c in evens:
-            for p in pieces:
-                if c != first_hop(p):
-                    kv_wait(p, c)
-                    pass_on(p, c)
-        for c in range(1, n, 2):
-            for p in pieces:
-                kv_wait(p, c)
+        here = b * n + me
+        evens = range(0, n, 2)
+        for count in range(n.bit_length() - 1):
+            group = [c for c in evens if bin(c).count("1") == count]
+            for c in group:
+                for p in pieces:
+                    if c and c != first_hop(p):
+                        kv_wait(p, c)
+                        pass_on(p, c)
+            for c in group:
+                for p in pieces:
+                    kv_wait(p, c | 1)
+                for one in (c, c | 1):
+                    g = b * n + (me ^ one)
+
+                    @pl.when((g <= here) & (g >= here - reach))
+                    def _():
+                        attend(b, b, g)
 
     def clear():
         m_s[...] = jnp.full_like(m_s, -1e30)
         l_s[...] = jnp.zeros_like(l_s)
         acc[...] = jnp.zeros_like(acc)
 
-    def attend(b, side):
+    def attend(b, side, only=None):
         here = b * n + me
         q = q_ref[b * rows : (b + 1) * rows]
 
@@ -297,6 +306,9 @@
             m_s[...] = new
             return carry
 
+        if only is not None:
+            piece(only, 0)
+            return
         low = jnp.maximum(here - reach, side * n)
         high = jnp.minimum(here, side * n + n - 1)
         lax.fori_loop(low, high + 1, piece, 0)
@@ -335,8 +347,7 @@
                 kv_wait(p, first_hop(p))
                 pass_on(p, first_hop(p))
             attend(b, b - 1)
-        gather_rest(b)
-        attend(b, b)
+        gather_attend(b)
         head_copies.append(finish(b, *((f1, f3, f2) if b == 0 else (o1, o3, o2))))
     for b in range(blocks):
         for copy in head_copies[b]:

time: 123 us -> 124 us (level)
  the two profiles are of different devices: /device:TPU:14 before, /device:TPU:15 now
where the time goes in v3:
time: 124 us; the launch traced here: 123 us
  Pallas kernels  117 us (94%)
  local copies, waits for them, and re-layouts  6.25 us (5%)
    pallas_call x1, Pallas kernels, mix(): pl.pallas_call(functools.partial(mix_kernel, n, nh, blocks), in_specs=[VM...  106 us
    pallas_call x1, Pallas kernels, project(): pl.pallas_call(functools.partial(project_kernel, rows), grid=(3,), in_spe...  10.5 us
    unnamed x8, local copies, waits for them, and re-layouts  6.25 us

profile of v3, /device:TPU:15, one launch (start us, length us, event | category | flops | bytes accessed | tf_op | source)
XLA Modules:
  0.0 123.4 jit_solution(16457644058371944996)
XLA Ops:
  0.6 10.5 %project.1 = (bf16[512,512]{1,0:T(8,128)(2,1)}, bf16[512,1024]{1,0:T(8,128)(2,1)}, bf16[3,512,512]{2,1,0:T(8,128)(2,1)}) custom-call(bf16[512,2048]{1,0:T(8,128)(2,1)} %bitcast.21, bf16[2048,1536]{1,0:T(8,128)(2,1)} %bitcast.20, bf16[1,2048]{1,0:T(2,128)(2,1)} %bitcast.22, f32[512,512]{1,0:T(8,128)} %bitcast.11, f32[512,512]{1,0:T(8,128)} %bitcast.13, ...), custom_call_target="tpu_custom_call" | custom-call | flops 3221225472 | bytes 6291456 | tf_op jit(solution)/shard_map/project/pallas_call | solution.py:77
  11.1 106.0 %mix.1 = (bf16[2,256,512]{2,1,0:T(8,128)(2,1)}, f32[512,512]{1,0:T(8,128)}, f32[512,512]{1,0:T(8,128)}, f32[512,512]{1,0:T(8,128)}) custom-call(bf16[512,512]{1,0:T(8,128)(2,1)} %get-tuple-element.11.q_ref, bf16[512,1024]{1,0:T(8,128)(2,1)} %get-tuple-element.12.kv_ref, bf16[3,512,512]{2,1,0:T(8,128)(2,1)} %get-tuple-element.13.g_ref, f32[512,512]{1,0:T(8,128)} %bitcast.12, ...), custom_call_target="tpu_custom_call" | custom-call | tf_op jit(solution)/shard_map/mix/pallas_call | solution.py:369
  117.2 0.0 copy-start.1
  117.2 2.0 %copy.16 = bf16[2,256,512]{2,1,0:T(8,128)(2,1)} copy(bf16[2,256,512]{2,1,0:T(8,128)(2,1)} %get-tuple-element.22) | data formatting | bytes 1048576
  119.1 0.0 copy-start
  119.1 2.4 %copy.17 = f32[1,512,512]{2,1,0:T(8,128)} copy(f32[1,512,512]{2,1,0:T(8,128)} %bitcast.19) | data formatting | bytes 2097152
  121.5 0.0 copy-done.1
  121.5 1.0 copy.18
  122.4 0.0 copy-done
  122.5 1.0 copy.19
Async XLA Ops:
  117.2 4.3 %copy-start.1 = (f32[512,512]{1,0:T(8,128)S(1)}, f32[512,512]{1,0:T(8,128)}, u32[]{:S(2)}) copy-start(f32[512,512]{1,0:T(8,128)} %get-tuple-element.16) | copy-start | bytes 3145732
  119.1 3.3 %copy-start = (f32[512,512]{1,0:T(8,128)S(1)}, f32[512,512]{1,0:T(8,128)}, u32[]{:S(2)}) copy-start(f32[512,512]{1,0:T(8,128)} %get-tuple-element.17) | copy-start | bytes 3145732
